TPU v7x, 8 devices: a whole 2x2x1 slice. The times are simulated.
8 devices in a mesh: rep: 2 (over z, y), grp: 4 (over x, core).
Axes of the slice: x: 2, y: 2, z: 1, core: 2. Of those that a mesh axis runs over, the one named last changes fastest.
Arguments:
- x_in: bfloat16 [512, 3584], P(('rep', 'grp')), parts along dimension 0
- seq_len: int32 [512], P(('rep', 'grp')), parts along dimension 0
- k_cache: bfloat16 [512, 256, 4, 128], P(('rep', 'grp')), parts along dimension 0
- v_cache: bfloat16 [512, 256, 4, 128], P(('rep', 'grp')), parts along dimension 0
- gamma_attn: bfloat16 [3584], replicated
- w_qkv: bfloat16 [3584, 4608], replicated
- b_qkv: bfloat16 [4608], replicated
- w_proj: bfloat16 [3584, 3584], replicated
- gamma_mlp: bfloat16 [3584], replicated
- w_in: bfloat16 [2, 18944, 3584], P(None, 'grp')
- w_out: bfloat16 [18944, 3584], P('grp')
Outputs:
- output 1: bfloat16 [512, 3584], P(('rep', 'grp')), parts along dimension 0
- output 2: bfloat16 [512, 256, 4, 128], P(('rep', 'grp')), parts along dimension 0
- output 3: bfloat16 [512, 256, 4, 128], P(('rep', 'grp')), parts along dimension 0
There are 2 independent parts. A program takes and returns all parts, laid end to end along the dimension named above; an argument that names none is the same for every part.
All inputs are finite; a program needn't handle non-finite values.
Results may differ from a plain program's by a relative error of at most 0.00754008.
Values are sent between devices in bfloat16 or wider.
A program may use at most 1 GiB of HBM per device.

v0:
```python
import jax
import jax.numpy as jnp
from jax import lax
from jax.sharding import PartitionSpec as P

HEAD_DIM = 128
ROPE_BASE = 10000.0
EPS = 1e-5


def rms_norm(vals, gain):
    mean_sq = jnp.mean(vals * vals, axis=-1, keepdims=True)
    return (vals * lax.rsqrt(mean_sq + EPS) * gain.astype(jnp.float32)).astype(jnp.bfloat16)


def rotary(vals, positions):
    rot_dim = HEAD_DIM // 2
    inv_freq = ROPE_BASE ** (-jnp.arange(0, rot_dim, 2, dtype=jnp.float32) / rot_dim)
    angles = positions.astype(jnp.float32)[:, None] * inv_freq[None, :]
    cosine = jnp.cos(angles)[:, None, :]
    sine = jnp.sin(angles)[:, None, :]
    pairs = vals[..., :rot_dim].reshape(vals.shape[:-1] + (rot_dim // 2, 2))
    even_part = pairs[..., 0]
    odd_part = pairs[..., 1]
    rotated = jnp.stack([even_part * cosine - odd_part * sine, odd_part * cosine + even_part * sine], axis=-1)
    return jnp.concatenate([rotated.reshape(vals.shape[:-1] + (rot_dim,)), vals[..., rot_dim:]], axis=-1)


def attention_block(x_in, seq_len, k_cache, v_cache, gamma_attn, w_qkv, b_qkv, w_proj):
    batch_rows, cache_len, kv_heads = k_cache.shape[0], k_cache.shape[1], k_cache.shape[2]
    num_heads = w_proj.shape[0] // HEAD_DIM
    q_width = num_heads * HEAD_DIM
    kv_width = kv_heads * HEAD_DIM
    x_f32 = x_in.astype(jnp.float32)
    normed = rms_norm(x_f32, gamma_attn)
    qkv_proj = jnp.dot(normed, w_qkv, preferred_element_type=jnp.float32) + b_qkv.astype(jnp.float32)
    query_rot = rotary(qkv_proj[:, :q_width].reshape(batch_rows, num_heads, HEAD_DIM), seq_len).astype(jnp.bfloat16)
    key_new = rotary(qkv_proj[:, q_width:q_width + kv_width].reshape(batch_rows, kv_heads, HEAD_DIM), seq_len).astype(jnp.bfloat16)
    value_new = qkv_proj[:, q_width + kv_width:].reshape(batch_rows, kv_heads, HEAD_DIM).astype(jnp.bfloat16)
    positions = jnp.arange(cache_len, dtype=jnp.int32)
    at_len = (positions[None, :] == seq_len[:, None])[:, :, None, None]
    k_out = jnp.where(at_len, key_new[:, None], k_cache)
    v_out = jnp.where(at_len, value_new[:, None], v_cache)
    q_grouped = query_rot.reshape(batch_rows, kv_heads, num_heads // kv_heads, HEAD_DIM)
    attn_scores = jnp.einsum('bgqd,blgd->bgql', q_grouped, k_out, preferred_element_type=jnp.float32) * HEAD_DIM ** -0.5
    visible = (positions[None, :] <= seq_len[:, None])[:, None, None, :]
    attn_probs = jax.nn.softmax(jnp.where(visible, attn_scores, -jnp.inf), axis=-1).astype(jnp.bfloat16)
    context = jnp.einsum('bgql,blgd->bgqd', attn_probs, v_out, preferred_element_type=jnp.float32)
    context = context.astype(jnp.bfloat16).reshape(batch_rows, q_width)
    hidden = x_f32 + jnp.dot(context, w_proj, preferred_element_type=jnp.float32)
    return hidden, k_out, v_out


def solution(mesh):
    row_spec = P(('rep', 'grp'))
    repl_spec = P()

    def local_layer(x_in, seq_len, k_cache, v_cache, gamma_attn, w_qkv, b_qkv, w_proj, gamma_mlp, w_in, w_out):
        hidden, k_out, v_out = attention_block(x_in, seq_len, k_cache, v_cache, gamma_attn, w_qkv, b_qkv, w_proj)
        mlp_in = rms_norm(hidden, gamma_mlp)
        group_rows = lax.all_gather(mlp_in, 'grp', axis=0, tiled=True)
        gate_up = jnp.einsum('bh,cfh->bcf', group_rows, w_in, preferred_element_type=jnp.float32)
        swiglu = (jax.nn.silu(gate_up[:, 0]) * gate_up[:, 1]).astype(jnp.bfloat16)
        part_sum = jnp.dot(swiglu, w_out, preferred_element_type=jnp.float32).astype(jnp.bfloat16)
        mlp_out = lax.psum_scatter(part_sum, 'grp', scatter_dimension=0, tiled=True)
        layer_out = (hidden + mlp_out.astype(jnp.float32)).astype(jnp.bfloat16)
        return layer_out, k_out, v_out

    return jax.shard_map(local_layer, mesh=mesh,
                         in_specs=(row_spec, row_spec, row_spec, row_spec, repl_spec, repl_spec, repl_spec,
                                   repl_spec, repl_spec, P(None, 'grp', None), P('grp', None)),
                         out_specs=(row_spec, row_spec, row_spec), check_vma=False)
```

profile of v0, /device:TPU:0, one launch (start us, length us, event | category | flops | bytes accessed | tf_op | source)
XLA Modules:
  0.0 194.6 jit_solution(1455978741932145175)
XLA Ops:
  7.2 0.7 convert_element_type.59
  7.9 0.7 iota_compare_fusion.1
  8.6 1.2 fusion.19
  9.9 0.7 convert_element_type.56
  10.6 0.7 convert_element_type.58
  11.3 13.6 %convolution_add_fusion = f32[64,4608]{1,0:T(8,128)S(1)} fusion(bf16[3584,4608]{1,0:T(8,128)(2,1)} %param.16, f32[4608]{0:T(1024)S(1)} %convert_element_type.58, bf16[64,3584]{1,0:T(8,128)(2,1)} %param.11, f32[3584]{0:T(1024)S(1)} %convert_element_type.56, f32[64]{0:T(128)S(1)} %add_rsqrt_fusion.1), kind=kOutput, calls=%fused_computation.7 | convolution fusion | flops 2115141632 | bytes 34701568 | tf_op jit(solution)/shard_map/dot_general | solution.py:36
  25.3 0.2 reshape.162
  26.4 0.2 slice.88
  26.7 0.3 copy.37
  27.1 0.6 copy.34
  27.6 1.2 subtract_convert_fusion
  28.8 1.2 pad_maximum_fusion
  30.0 0.8 copy.36
  30.8 25.9 %broadcast_select_fusion.1 = (bf16[64,256,4,128]{3,2,1,0:T(4,128)(2,1)}, bf16[64,256,4,128]{3,2,1,0:T(4,128)(2,1)}) fusion(bf16[64,256,4,128]{3,2,1,0:T(4,128)(2,1)} %param.13, pred[64,256]{1,0:T(8,128)(4,1)S(1)} %get-tuple-element.12, bf16[64,4,128]{2,1,0:T(4,128)(2,1)S(1)} %copy.41, bf16[64,256,4,128]{3,2,1,0:T(4,128)(2,1)} %param.14, ...), kind=kLoop, calls=%fused_computation.6 | loop fusion | flops 16777216 | bytes 67256320 | tf_op jit(solution)/shard_map/jit(_where)/select_n | solution.py:42
  56.7 11.8 %fusion.32 = (f32[64,4,7]{2,1,0:T(4,128)S(1)}, f32[64,4,7,256]{3,2,1,0:T(8,128)}) fusion(pred[64,256]{1,0:T(8,128)(4,1)S(1)} %get-tuple-element.11, bf16[64,256,4,128]{3,2,1,0:T(4,128)(2,1)} %get-tuple-element.7, bf16[64,4,7,64]{3,2,1,0:T(8,128)(2,1)S(1)} %copy.37, bf16[64,4,7,64]{3,2,1,0:T(8,128)(2,1)S(1)} %copy.36), kind=kOutput, calls=%fused_computation.60 | convolution fusion | flops 120193280 | bytes 19094528 | tf_op jit(solution)/shard_map/sub | solution.py:47
  68.5 8.8 %fusion.12 = bf16[64,4,7,128]{3,2,1,0:T(8,128)(2,1)S(1)} fusion(bf16[64,256,4,128]{3,2,1,0:T(4,128)(2,1)} %get-tuple-element.8, f32[64,4,7,256]{3,2,1,0:T(8,128)} %get-tuple-element.14, f32[64,4,7]{2,1,0:T(4,128)S(1)} %get-tuple-element.13), kind=kOutput, calls=%fused_computation.23 | convolution fusion | flops 118587392 | bytes 19078144 | tf_op jit(solution)/shard_map/bgql,blgd->bgqd/dot_general | solution.py:48
  77.3 0.5 reshape.166
  77.8 10.8 %multiply_reduce_fusion = (f32[64]{0:T(128)S(1)}, f32[64,3584]{1,0:T(8,128)S(1)}) fusion(bf16[64,3584]{1,0:T(8,128)(2,1)S(1)} %reshape.166, bf16[3584,3584]{1,0:T(8,128)(2,1)} %param.18, bf16[64,3584]{1,0:T(8,128)(2,1)S(1)} %copy-done), kind=kOutput, calls=%fused_computation.34 | convolution fusion | flops 1645084672 | bytes 27525376 | tf_op jit(solution)/shard_map/dot_general | solution.py:50
  88.6 0.9 multiply_convert_fusion
  89.6 21.0 %all-gather.2.cloned.1.call-done = bf16[256,3584]{1,0:T(8,128)(2,1)} async-done(((bf16[64,3584]{1,0:T(8,128)(2,1)}), bf16[256,3584]{1,0:T(8,128)(2,1)}) %all-gather.2.cloned.1.call-update) | async-done | bytes 1835024 | tf_op jit(solution)/shard_map/all_gather | solution.py:61
  110.6 30.5 %fusion.10 = f32[256,2,4736]{2,0,1:T(8,128)} fusion(bf16[2,4736,3584]{2,1,0:T(8,128)(2,1)} %param.20, bf16[256,3584]{1,0:T(8,128)(2,1)} %all-gather.2.cloned.1.call-done), kind=kOutput, calls=%fused_computation.19 | convolution fusion | flops 17381195776 | bytes 79429632 | tf_op jit(solution)/shard_map/bh,cfh->bcf/dot_general | solution.py:62
  141.1 20.6 %convolution_convert_fusion = bf16[256,3584]{1,0:T(8,128)(2,1)} fusion(bf16[4736,3584]{1,0:T(8,128)(2,1)} %param.21, f32[256,2,4736]{2,0,1:T(8,128)} %fusion.10), kind=kOutput, calls=%fused_computation.8 | convolution fusion | flops 8698789888 | bytes 45481984 | tf_op jit(solution)/shard_map/dot_general | solution.py:64
  161.8 24.1 %reduce-scatter.2.cloned.1.call-done = bf16[64,3584]{1,0:T(8,128)(2,1)} async-done(((bf16[256,3584]{1,0:T(8,128)(2,1)}), bf16[64,3584]{1,0:T(8,128)(2,1)}) %reduce-scatter.2.cloned.1.call-update) | async-done | bytes 458768 | tf_op jit(solution)/shard_map/reduce_scatter | solution.py:65
  185.9 1.9 add_convert_fusion
  (27 shorter events, 1.4 us)
Async XLA Ops:
  7.2 103.5 %all-gather.2.cloned.1.call-start = ((), (), s32[]{:S(2)}) async-start(), calls=%async_computation.1 | async-start | bytes 2293760 | tf_op jit(solution)/shard_map/all_gather | solution.py:61
  11.3 13.8 %copy-start.1 = (bf16[3584]{0:T(1024)(128)(2,1)S(1)}, bf16[3584]{0:T(1024)(128)(2,1)}, u32[]{:S(2)}) copy-start(bf16[3584]{0:T(1024)(128)(2,1)} %param.19) | copy-start | bytes 21508
  68.5 9.3 %copy-start = (bf16[64,3584]{1,0:T(8,128)(2,1)S(1)}, bf16[64,3584]{1,0:T(8,128)(2,1)}, u32[]{:S(2)}) copy-start(bf16[64,3584]{1,0:T(8,128)(2,1)} %param.11) | copy-start | bytes 1376260
  89.6 96.3 %reduce-scatter.2.cloned.1.call-start = ((), (), s32[]{:S(2)}) async-start(), calls=%async_computation.2 | async-start | bytes 2293760 | tf_op jit(solution)/shard_map/reduce_scatter | solution.py:65
Sparse Core Ops, SparseCore 0:
  89.7 20.9 all-gather.1
  161.9 23.9 reduce-scatter.1
where the time goes:
time: 195 us
  matrix products  96.1 us (49%)
  waiting for transfers between devices  45.1 us (23%)
  other arithmetic  35.7 us (18%)
  between operations  14.3 us (7%)
  local copies, waits for them, and re-layouts  3.25 us (2%)
    dot_general x1, matrix products, local_layer(): jnp.einsum('bh,cfh->bcf', group_rows, w_in, preferred_element_type=jnp.fl...  30.5 us
    select_n x1, other arithmetic, attention_block(): k_out = jnp.where(at_len, key_new[:, None], k_cache)  25.9 us
    reduce_scatter x1, waiting for transfers between devices, local_layer(): mlp_out = lax.psum_scatter(part_sum, 'grp', scatter_dimension=0, tiled=True)  24.1 us
    all_gather x1, waiting for transfers between devices, local_layer(): group_rows = lax.all_gather(mlp_in, 'grp', axis=0, tiled=True)  21 us
    dot_general x1, matrix products, local_layer(): jnp.dot(swiglu, w_out, preferred_element_type=jnp.float32)  20.6 us
    dot_general x1, matrix products, attention_block(): jnp.dot(normed, w_qkv, preferred_element_type=jnp.float32)  13.6 us
    sub x1, matrix products, attention_block(): jax.nn.softmax(jnp.where(visible, attn_scores, -jnp.inf), axis=-1)  11.8 us
    dot_general x1, matrix products, attention_block(): jnp.dot(context, w_proj, preferred_element_type=jnp.float32)  10.8 us
  transfers between devices with their start and end apart: 2, of which 2 were waited for; matrix products, arithmetic and copies ran while one was open for 0% of the time, Pallas kernels for 0%

commit v1 on v0

v1 whole, which is shorter than its diff:
```python
import functools

import jax
import jax.numpy as jnp
from jax import lax
from jax.experimental import pallas as pl
from jax.experimental.pallas import tpu as pltpu
from jax.sharding import PartitionSpec as P

HEAD = 128
ROPE_BASE = 10000.0
EPS = 1e-5
MESH = pl.DeviceIdType.MESH
F32 = jnp.float32
BF16 = jnp.bfloat16
LOG2E = 1.4426950408889634

QKV_COLS = 512
QKV_SLOTS = 4
SEQ_STEP = 4
SEQ_SLOTS = 4
HEAD_ROWS = 32
FF_BLOCK = 256
FF_SLOTS = 7
OUT_COLS = 512
OUT_SLOTS = 5
AG_CHUNKS = 4


def rms_norm(vals, gain):
    mean_sq = jnp.mean(vals * vals, axis=-1, keepdims=True)
    return (vals * lax.rsqrt(mean_sq + EPS) * gain.astype(F32)).astype(BF16)


def qkv_attention_kernel(q_heads, kv_heads, len_ref, x_ref, gain_ref, bias_ref, cos_ref, sin_ref, w_hbm, k_hbm, v_hbm,
                         ctx_ref, ko_hbm, vo_hbm, wbuf, kbuf, vbuf, n_scr, q_scr, kn_scr, vn_scr,
                         w_sem, ki_sem, vi_sem, ko_sem, vo_sem):
    rows = x_ref.shape[0]
    blocks = w_hbm.shape[1] // QKV_COLS
    steps = rows // SEQ_STEP
    group = q_heads // kv_heads
    heads_per_block = QKV_COLS // HEAD

    def w_copy(i):
        return pltpu.make_async_copy(w_hbm.at[:, pl.ds(i * QKV_COLS, QKV_COLS)], wbuf.at[i % QKV_SLOTS],
                                     w_sem.at[i % QKV_SLOTS])

    def in_copies(i):
        slot = lax.rem(i, SEQ_SLOTS)
        part = pl.ds(i * SEQ_STEP, SEQ_STEP)
        return (pltpu.make_async_copy(k_hbm.at[part], kbuf.at[slot], ki_sem.at[slot]),
                pltpu.make_async_copy(v_hbm.at[part], vbuf.at[slot], vi_sem.at[slot]))

    def out_copies(i):
        slot = lax.rem(i, SEQ_SLOTS)
        part = pl.ds(i * SEQ_STEP, SEQ_STEP)
        return (pltpu.make_async_copy(kbuf.at[slot], ko_hbm.at[part], ko_sem.at[slot]),
                pltpu.make_async_copy(vbuf.at[slot], vo_hbm.at[part], vo_sem.at[slot]))

    for i in range(QKV_SLOTS):
        w_copy(i).start()
    n_scr[...] = rms_norm(x_ref[...].astype(F32), gain_ref[...])
    q_scr[:, pl.ds(q_heads, HEAD_ROWS - q_heads), :] = jnp.zeros((rows, HEAD_ROWS - q_heads, HEAD), F32)
    even = lax.rem(lax.broadcasted_iota(jnp.int32, (rows, HEAD), 1), 2) == 0
    cosine = cos_ref[...]
    sine = sin_ref[...]

    for i in range(blocks):
        w_copy(i).wait()
        part = jnp.dot(n_scr[...], wbuf[i % QKV_SLOTS], preferred_element_type=F32)
        part = part + bias_ref[:, pl.ds(i * QKV_COLS, QKV_COLS)].astype(F32)
        if i + QKV_SLOTS < blocks:
            w_copy(i + QKV_SLOTS).start()
        elif i + QKV_SLOTS - blocks < 2:
            for copy in in_copies(i + QKV_SLOTS - blocks):
                copy.start()
        for j in range(heads_per_block):
            head = i * heads_per_block + j
            vals = part[:, j * HEAD:(j + 1) * HEAD]
            if head < q_heads + kv_heads:
                other = jnp.where(even, pltpu.roll(vals, HEAD - 1, 1), pltpu.roll(vals, 1, 1))
                vals = vals * cosine + other * sine
            if head < q_heads:
                q_scr[:, head, :] = vals
            elif head < q_heads + kv_heads:
                for rep in range(8 // kv_heads):
                    kn_scr[:, rep * kv_heads + head - q_heads, :] = vals
            else:
                for rep in range(8 // kv_heads):
                    vn_scr[:, rep * kv_heads + head - q_heads - kv_heads, :] = vals

    cols = kbuf.shape[2]
    col = lax.broadcasted_iota(jnp.int32, (HEAD_ROWS, cols), 1)
    row_group = jnp.minimum(lax.broadcasted_iota(jnp.int32, (HEAD_ROWS, cols), 0) // group, kv_heads - 1)
    own_group = lax.rem(col, kv_heads) == row_group
    positions = 16 // kv_heads

    def attend(i, carry):
        slot = lax.rem(i, SEQ_SLOTS)

        @pl.when(i >= 2)
        def _():
            for copy in out_copies(i - 2):
                copy.wait()

        @pl.when(i + 2 < steps)
        def _():
            for copy in in_copies(i + 2):
                copy.start()

        for copy in in_copies(i):
            copy.wait()
        lengths = [len_ref[i * SEQ_STEP + s] for s in range(SEQ_STEP)]
        new_row = lax.broadcasted_iota(jnp.int32, (16, HEAD), 0) // kv_heads
        for s in range(SEQ_STEP):
            base = pl.multiple_of((lengths[s] // positions) * 16, 16)
            hit = new_row == lax.rem(lengths[s], positions)
            for buf, new in ((kbuf, kn_scr), (vbuf, vn_scr)):
                fresh = new[i * SEQ_STEP + s]
                fresh = jnp.concatenate([fresh, fresh], axis=0).astype(BF16).astype(F32)
                old = buf[slot, s, pl.ds(base, 16), :].astype(F32)
                buf[slot, s, pl.ds(base, 16), :] = jnp.where(hit, fresh, old).astype(BF16)
        scores = [lax.dot_general(q_scr[i * SEQ_STEP + s].astype(BF16), kbuf[slot, s], (((1,), (1,)), ((), ())),
                                  preferred_element_type=F32) for s in range(SEQ_STEP)]
        for s in range(SEQ_STEP):
            seen = jnp.logical_and(own_group, col < (lengths[s] + 1) * kv_heads)
            logits = jnp.where(seen, scores[s] * (HEAD ** -0.5 * LOG2E), -jnp.inf)
            top = jnp.max(logits, axis=-1, keepdims=True)
            weights = jnp.exp2(logits - top)
            total = jnp.sum(weights, axis=-1, keepdims=True)
            probs = (weights * (1.0 / total)).astype(BF16)
            ctx_ref[i * SEQ_STEP + s] = jnp.dot(probs, vbuf[slot, s], preferred_element_type=F32)
        for copy in out_copies(i):
            copy.start()
        return carry

    lax.fori_loop(0, steps, attend, 0)
    for i in (steps - 2, steps - 1):
        for copy in out_copies(i):
            copy.wait()


def mlp_kernel(q_heads, ctx_ref, x_ref, gain_ref, wp_hbm, wi_hbm, wo_hbm, y_ref,
               ring, oring, m_all, ctx2, hid, act, send_d, recv_d, keep, send_i, recv_i,
               ring_sem, oring_sem, agx_s, agx_r, agp_s, agp_r, fwd_s, fwd_r, rsd_s, rsd_r, rsi_s, rsi_r):
    rows, width = x_ref.shape
    ffn = wo_hbm.shape[0]
    me = lax.axis_index("grp")
    partner = {"grp": me + 1 - 2 * lax.rem(me, 2)}
    cross = {"grp": lax.rem(me + 2, 4)}
    proj_blocks = wp_hbm.shape[0] // 2
    full = ffn // FF_BLOCK
    rest = ffn - full * FF_BLOCK
    chunks = width // OUT_COLS

    barrier = pltpu.get_barrier_semaphore()
    for peer in (partner, cross):
        pl.semaphore_signal(barrier, inc=1, device_id=peer, device_id_type=MESH)

    def proj_copy(i):
        return pltpu.make_async_copy(wp_hbm.at[pl.ds(2 * i, 2)], ring.at[i], ring_sem.at[i])

    def in_copy(j):
        slot = lax.rem(j, FF_SLOTS)
        return pltpu.make_async_copy(wi_hbm.at[:, pl.ds(pl.multiple_of(j * FF_BLOCK, FF_BLOCK), FF_BLOCK), :],
                                     ring.at[slot], ring_sem.at[slot])

    def rest_copy():
        slot = full % FF_SLOTS
        return pltpu.make_async_copy(wi_hbm.at[:, pl.ds(full * FF_BLOCK, rest), :],
                                     ring.at[slot, :, pl.ds(0, rest), :], ring_sem.at[slot])

    def out_copy(c):
        slot = lax.rem(c, OUT_SLOTS)
        return pltpu.make_async_copy(wo_hbm.at[:, pl.ds(pl.multiple_of(c * OUT_COLS, OUT_COLS), OUT_COLS)],
                                     oring.at[slot], oring_sem.at[slot])

    for i in range(proj_blocks):
        proj_copy(i).start()
    for head in range(q_heads):
        ctx2[:, pl.ds(head * HEAD, HEAD)] = ctx_ref[:, head, :].astype(BF16)
    hid[...] = x_ref[...].astype(F32)

    def project(i, carry):
        proj_copy(i).wait()
        block = ring[i].reshape(2 * FF_BLOCK, width)
        left = ctx2[:, pl.ds(pl.multiple_of(i * 2 * FF_BLOCK, 2 * FF_BLOCK), 2 * FF_BLOCK)]
        hid[...] += jnp.dot(left, block, preferred_element_type=F32)
        in_copy(i).start()
        return carry

    lax.fori_loop(0, proj_blocks, project, 0)
    out_copy(0).start()
    out_copy(1).start()
    m_all[pl.ds(0, rows), :] = rms_norm(hid[...], gain_ref[...])
    pl.semaphore_wait(barrier, 2)

    piece = rows // AG_CHUNKS

    def remote(src, dst, send, recv, peer):
        return pltpu.make_async_remote_copy(src_ref=src, dst_ref=dst, send_sem=send, recv_sem=recv,
                                            device_id=peer, device_id_type=MESH)

    to_cross = [remote(m_all.at[pl.ds(k * piece, piece)], m_all.at[pl.ds(rows + k * piece, piece)],
                       agx_s.at[k], agx_r.at[k], cross) for k in range(AG_CHUNKS)]
    to_partner = remote(m_all.at[pl.ds(0, rows)], m_all.at[pl.ds(2 * rows, rows)], agp_s, agp_r, partner)
    forward = [remote(m_all.at[pl.ds(rows + k * piece, piece)], m_all.at[pl.ds(3 * rows + k * piece, piece)],
                      fwd_s.at[k], fwd_r.at[k], partner) for k in range(AG_CHUNKS)]
    for copy in to_cross:
        copy.start()
    to_partner.start()
    for k in range(AG_CHUNKS):
        to_cross[k].wait_recv()
        forward[k].start()
    to_partner.wait_recv()
    for k in range(AG_CHUNKS):
        forward[k].wait_recv()

    def swiglu(gate, up):
        return (gate / (1.0 + jnp.exp(-gate)) * up).astype(BF16)

    contract_last = (((1,), (1,)), ((), ()))

    def gate_up(j, carry):
        slot = lax.rem(j, FF_SLOTS)
        in_copy(j).wait()
        gate = lax.dot_general(m_all[...], ring[slot, 0], contract_last, preferred_element_type=F32)
        up = lax.dot_general(m_all[...], ring[slot, 1], contract_last, preferred_element_type=F32)
        act[:, pl.ds(pl.multiple_of(j * FF_BLOCK, FF_BLOCK), FF_BLOCK)] = swiglu(gate, up)

        @pl.when(j + FF_SLOTS < full)
        def _():
            in_copy(j + FF_SLOTS).start()

        @pl.when(j + FF_SLOTS == full)
        def _():
            rest_copy().start()

        for c in range(2, OUT_SLOTS):
            @pl.when(j == 3 * (c - 1))
            def _():
                out_copy(c).start()

        return carry

    lax.fori_loop(0, full, gate_up, 0)
    rest_copy().wait()
    slot = full % FF_SLOTS
    gate = lax.dot_general(m_all[...], ring[slot, 0, pl.ds(0, rest), :], contract_last, preferred_element_type=F32)
    up = lax.dot_general(m_all[...], ring[slot, 1, pl.ds(0, rest), :], contract_last, preferred_element_type=F32)
    act[:, pl.ds(full * FF_BLOCK, rest)] = swiglu(gate, up)

    def die_copy(c):
        return remote(send_d.at[c], recv_d.at[c], rsd_s.at[c], rsd_r.at[c], partner)

    def chip_copy(c):
        return remote(send_i.at[c], recv_i.at[c], rsi_s.at[c], rsi_r.at[c], cross)

    def finish(c):
        cols = pl.ds(pl.multiple_of(c * OUT_COLS, OUT_COLS), OUT_COLS)
        die_copy(c).wait_recv()
        chip_sum = keep[lax.rem(c, 2)] + recv_d[c].astype(F32)
        send_i[c] = chip_sum[rows:].astype(BF16)
        hid[:, cols] += chip_sum[:rows]
        chip_copy(c).start()

    def down(c, carry):
        out_copy(c).wait()
        part = jnp.dot(act[...], oring[lax.rem(c, OUT_SLOTS)], preferred_element_type=F32)

        @pl.when(c + OUT_SLOTS < chunks)
        def _():
            out_copy(c + OUT_SLOTS).start()

        send_d[c] = part[2 * rows:].astype(BF16)
        keep[lax.rem(c, 2)] = part[:2 * rows]
        die_copy(c).start()

        @pl.when(c > 0)
        def _():
            finish(c - 1)

        return carry

    lax.fori_loop(0, chunks, down, 0)
    finish(chunks - 1)
    for c in range(chunks):
        cols = pl.ds(c * OUT_COLS, OUT_COLS)
        chip_copy(c).wait_recv()
        y_ref[:, cols] = (hid[:, cols] + recv_i[c].astype(F32)).astype(BF16)
    for copy in (*to_cross, to_partner, *forward):
        copy.wait_send()
    for c in range(chunks):
        die_copy(c).wait_send()
        chip_copy(c).wait_send()


def solution(mesh):
    row_spec = P(('rep', 'grp'))
    repl_spec = P()
    vmem = pl.BlockSpec(memory_space=pltpu.VMEM)
    smem = pl.BlockSpec(memory_space=pltpu.SMEM)
    hbm = pl.BlockSpec(memory_space=pl.ANY)
    dma = pltpu.SemaphoreType.DMA

    def local_layer(x_in, seq_len, k_cache, v_cache, gamma_attn, w_qkv, b_qkv, w_proj, gamma_mlp, w_in, w_out):
        rows, width = x_in.shape
        cache_len, kv_heads = k_cache.shape[1:3]
        q_heads = w_proj.shape[0] // HEAD
        ffn = w_out.shape[0]
        cache_rows = cache_len * kv_heads

        rot_dim = HEAD // 2
        inv_freq = ROPE_BASE ** (-jnp.arange(0, rot_dim, 2, dtype=F32) / rot_dim)
        angles = seq_len.astype(F32)[:, None] * jnp.repeat(inv_freq, 2)[None, :]
        sign = jnp.where(jnp.arange(rot_dim) % 2 == 0, -1.0, 1.0).astype(F32)
        cosine = jnp.concatenate([jnp.cos(angles), jnp.ones((rows, HEAD - rot_dim), F32)], axis=1)
        sine = jnp.concatenate([jnp.sin(angles) * sign, jnp.zeros((rows, HEAD - rot_dim), F32)], axis=1)

        flat = jax.ShapeDtypeStruct((rows, cache_rows, HEAD), BF16)
        context, k_out, v_out = pl.pallas_call(
            functools.partial(qkv_attention_kernel, q_heads, kv_heads),
            out_shape=(jax.ShapeDtypeStruct((rows, HEAD_ROWS, HEAD), F32), flat, flat),
            in_specs=[smem, vmem, vmem, vmem, vmem, vmem, hbm, hbm, hbm],
            out_specs=(vmem, hbm, hbm),
            scratch_shapes=[
                pltpu.VMEM((QKV_SLOTS, width, QKV_COLS), BF16),
                pltpu.VMEM((SEQ_SLOTS, SEQ_STEP, cache_rows, HEAD), BF16),
                pltpu.VMEM((SEQ_SLOTS, SEQ_STEP, cache_rows, HEAD), BF16),
                pltpu.VMEM((rows, width), BF16),
                pltpu.VMEM((rows, HEAD_ROWS, HEAD), F32),
                pltpu.VMEM((rows, 8, HEAD), F32),
                pltpu.VMEM((rows, 8, HEAD), F32),
                dma((QKV_SLOTS,)), dma((SEQ_SLOTS,)), dma((SEQ_SLOTS,)), dma((SEQ_SLOTS,)), dma((SEQ_SLOTS,)),
            ],
            compiler_params=pltpu.CompilerParams(vmem_limit_bytes=60 * 1024 * 1024),
            name="qkv_attention",
        )(seq_len, x_in, gamma_attn.reshape(1, width), b_qkv.reshape(1, -1), cosine, sine, w_qkv,
          k_cache.reshape(rows, cache_rows, HEAD), v_cache.reshape(rows, cache_rows, HEAD))

        chunks = width // OUT_COLS
        layer_out = pl.pallas_call(
            functools.partial(mlp_kernel, q_heads),
            out_shape=jax.ShapeDtypeStruct((rows, width), BF16),
            in_specs=[vmem, vmem, vmem, hbm, hbm, hbm],
            out_specs=vmem,
            scratch_shapes=[
                pltpu.VMEM((FF_SLOTS, 2, FF_BLOCK, width), BF16),
                pltpu.VMEM((OUT_SLOTS, ffn, OUT_COLS), BF16),
                pltpu.VMEM((4 * rows, width), BF16),
                pltpu.VMEM((rows, width), BF16),
                pltpu.VMEM((rows, width), F32),
                pltpu.VMEM((4 * rows, ffn), BF16),
                pltpu.VMEM((chunks, 2 * rows, OUT_COLS), BF16),
                pltpu.VMEM((chunks, 2 * rows, OUT_COLS), BF16),
                pltpu.VMEM((2, 2 * rows, OUT_COLS), F32),
                pltpu.VMEM((chunks, rows, OUT_COLS), BF16),
                pltpu.VMEM((chunks, rows, OUT_COLS), BF16),
                dma((FF_SLOTS,)), dma((OUT_SLOTS,)),
                dma((AG_CHUNKS,)), dma((AG_CHUNKS,)), dma, dma, dma((AG_CHUNKS,)), dma((AG_CHUNKS,)),
                dma((chunks,)), dma((chunks,)), dma((chunks,)), dma((chunks,)),
            ],
            compiler_params=pltpu.CompilerParams(collective_id=0, has_side_effects=True,
                                                 vmem_limit_bytes=67043328),
            name="proj_mlp",
        )(context, x_in, gamma_mlp.reshape(1, width), w_proj.reshape(-1, FF_BLOCK, width), w_in, w_out)
        return layer_out, k_out.reshape(k_cache.shape), v_out.reshape(v_cache.shape)

    return jax.shard_map(local_layer, mesh=mesh,
                         in_specs=(row_spec, row_spec, row_spec, row_spec, repl_spec, repl_spec, repl_spec,
                                   repl_spec, repl_spec, P(None, 'grp', None), P('grp', None)),
                         out_specs=(row_spec, row_spec, row_spec), check_vma=False)
```

time: 195 us -> 108 us (0.55)
  Pallas kernels: 0 us -> 98.5 us
  matrix products: 96.1 us -> 0 us
  waiting for transfers between devices: 45.1 us -> 0 us
  other arithmetic: 35.7 us -> 0.87 us
  between operations: 14.3 us -> 0.66 us
  local copies, waits for them, and re-layouts: 3.25 us -> 7.16 us
    pallas_call x0 -> x2, Pallas kernels: none -> 98.5 us  [the longest x1 63 us: local_layer(): pl.pallas_call(functools.partial(mlp_kernel, q_heads), out_shape=jax.Shap...]
    dot_general x5 -> x0, matrix products: 84.3 us -> none  [the longest x1 30.5 us: local_layer(): jnp.einsum('bh,cfh->bcf', group_rows, w_in, preferred_element_type=jnp.fl...]
    select_n x1, other arithmetic: 25.9 us -> 0.01 us  [local_layer(): sign = jnp.where(jnp.arange(rot_dim) % 2 == 0, -1.0, 1.0).astype(F32)]
    reduce_scatter x1 -> x0, waiting for transfers between devices: 24.1 us -> none  [local_layer(): mlp_out = lax.psum_scatter(part_sum, 'grp', scatter_dimension=0, tiled=True)]
    all_gather x1 -> x0, waiting for transfers between devices: 21 us -> none  [local_layer(): group_rows = lax.all_gather(mlp_in, 'grp', axis=0, tiled=True)]
    sub x1 -> x0, matrix products: 11.8 us -> none  [attention_block(): jax.nn.softmax(jnp.where(visible, attn_scores, -jnp.inf), axis=-1)]
    convert_element_type x6 -> x1, other arithmetic: 4.87 us -> 0.66 us  [local_layer(): angles = seq_len.astype(F32)[:, None] * jnp.repeat(inv_freq, 2)[None, :]]
    reshape x3, local copies, waits for them, and re-layouts: 0.75 us -> 3.94 us  [the longest x1 1.32 us: local_layer(): b_qkv.reshape(1, -1)]
  transfers between devices with their start and end apart: 2 -> 0, of which waited for: 2 -> 0; matrix products, arithmetic and copies ran while one was open for 0% -> 0% of each run, Pallas kernels for 0% -> 0%
where the time goes in v1:
time: 108 us; the launch traced here: 107 us
  Pallas kernels  98.5 us (91%)
  local copies, waits for them, and re-layouts  7.16 us (7%)
    pallas_call x1, Pallas kernels, local_layer(): pl.pallas_call(functools.partial(mlp_kernel, q_heads), out_shape=jax.Shap...  63 us
    pallas_call x1, Pallas kernels, local_layer(): pl.pallas_call(functools.partial(qkv_attention_kernel, q_heads, kv_heads)...  35.6 us

profile of v1, /device:TPU:0, one launch (start us, length us, event | category | flops | bytes accessed | tf_op | source)
XLA Modules:
  0.0 107.2 jit_solution(13716763194591960669)
XLA Ops:
  0.6 0.7 convert_element_type.3
  1.3 1.3 %reshape.43.gain_ref = bf16[1,3584]{1,0:T(2,128)(2,1)} reshape(bf16[3584]{0:T(1024)(128)(2,1)} %param.15) | data formatting | bytes 14336 | tf_op jit(solution)/shard_map/reshape | solution.py:338
  2.6 1.3 %reshape.47.gain_ref = bf16[1,3584]{1,0:T(2,128)(2,1)} reshape(bf16[3584]{0:T(1024)(128)(2,1)} %param.19) | data formatting | bytes 14336 | tf_op jit(solution)/shard_map/reshape | solution.py:366
  3.9 0.1 broadcast_in_dim.15
  4.0 0.1 mul.32
  4.1 1.3 %reshape.44.bias_ref = bf16[1,4608]{1,0:T(2,128)(2,1)} reshape(bf16[4608]{0:T(1024)(128)(2,1)} %param.17) | data formatting | bytes 18432 | tf_op jit(solution)/shard_map/reshape | solution.py:338
  5.4 0.2 fusion
  5.6 0.6 concatenate.7.sin_ref
  6.2 0.6 concatenate.6.cos_ref
  6.9 35.6 %qkv_attention.1 = (f32[64,32,128]{2,1,0:T(8,128)}, bf16[64,1024,128]{2,1,0:T(8,128)(2,1)}, bf16[64,1024,128]{2,1,0:T(8,128)(2,1)}) custom-call(s32[64]{0:T(128)} %len_ref.1, bf16[64,3584]{1,0:T(8,128)(2,1)} %x_ref.3, bf16[1,3584]{1,0:T(2,128)(2,1)} %reshape.43.gain_ref, bf16[1,4608]{1,0:T(2,128)(2,1)} %reshape.44.bias_ref, f32[64,128]{1,0:T(8,128)} %concatenate.6.cos_ref, ...), custom_call_target="tpu_custom_call" | custom-call | tf_op jit(solution)/shard_map/qkv_attention/pallas_call | solution.py:321
  42.4 63.0 %proj_mlp.1 = bf16[64,3584]{1,0:T(8,128)(2,1)} custom-call(f32[64,32,128]{2,1,0:T(8,128)} %get-tuple-element.6.ctx_ref, bf16[64,3584]{1,0:T(8,128)(2,1)} %x_ref.3, bf16[1,3584]{1,0:T(2,128)(2,1)} %reshape.47.gain_ref, bf16[14,256,3584]{2,1,0:T(8,128)(2,1)} %bitcast.5, bf16[2,4736,3584]{2,1,0:T(8,128)(2,1)} %wi_hbm.1, bf16[4736,3584]{1,0:T(8,128)(2,1)} %wo_hbm.1), custom_call_target="tpu_custom_call" | custom-call | tf_op jit(solution)/shard_map/proj_mlp/pallas_call | solution.py:342
  105.4 1.8 %copy.15 = bf16[64,3584]{1,0:T(8,128)(2,1)} copy(bf16[64,3584]{1,0:T(8,128)(2,1)} %proj_mlp.1) | data formatting | bytes 917504
  (2 shorter events, 0.0 us)

commit v2 on v1

--- a/solution.py
+++ b/solution.py
@@ -1,4 +1,5 @@
 import functools
+import math
 
 import jax
 import jax.numpy as jnp
@@ -22,6 +23,7 @@
 HEAD_ROWS = 32
 FF_BLOCK = 256
 FF_SLOTS = 7
+FF_UNROLL = 3
 OUT_COLS = 512
 OUT_SLOTS = 5
 AG_CHUNKS = 4
@@ -29,11 +31,23 @@
 
 def rms_norm(vals, gain):
     mean_sq = jnp.mean(vals * vals, axis=-1, keepdims=True)
-    return (vals * lax.rsqrt(mean_sq + EPS) * gain.astype(F32)).astype(BF16)
-
-
-def qkv_attention_kernel(q_heads, kv_heads, len_ref, x_ref, gain_ref, bias_ref, cos_ref, sin_ref, w_hbm, k_hbm, v_hbm,
-                         ctx_ref, ko_hbm, vo_hbm, wbuf, kbuf, vbuf, n_scr, q_scr, kn_scr, vn_scr,
+    return (vals * lax.rsqrt(mean_sq + EPS) * gain.astype(F32).reshape(1, -1)).astype(BF16)
+
+
+def rotary_tables(len_ref, table, rows):
+    rot_dim = HEAD // 2
+    for b in range(rows):
+        table[pl.ds(b, 1), :] = jnp.full((1, HEAD), len_ref[b], jnp.int32).astype(F32)
+    dim = lax.broadcasted_iota(jnp.int32, (1, HEAD), 1)
+    pair = (dim // 2 * 2).astype(F32)
+    inv_freq = jnp.where(dim < rot_dim, jnp.exp(pair * (-math.log(ROPE_BASE) / rot_dim)), 0.0)
+    angles = table[...] * inv_freq
+    sine = jnp.sin(angles)
+    return jnp.cos(angles), jnp.where(lax.rem(dim, 2) == 0, -sine, sine)
+
+
+def qkv_attention_kernel(q_heads, kv_heads, len_ref, x_ref, gain_ref, bias_ref, w_hbm, k_hbm, v_hbm,
+                         ctx_ref, ko_hbm, vo_hbm, wbuf, kbuf, vbuf, table, n_scr, q_scr, kn_scr, vn_scr,
                          w_sem, ki_sem, vi_sem, ko_sem, vo_sem):
     rows = x_ref.shape[0]
     blocks = w_hbm.shape[1] // QKV_COLS
@@ -62,13 +76,12 @@
     n_scr[...] = rms_norm(x_ref[...].astype(F32), gain_ref[...])
     q_scr[:, pl.ds(q_heads, HEAD_ROWS - q_heads), :] = jnp.zeros((rows, HEAD_ROWS - q_heads, HEAD), F32)
     even = lax.rem(lax.broadcasted_iota(jnp.int32, (rows, HEAD), 1), 2) == 0
-    cosine = cos_ref[...]
-    sine = sin_ref[...]
+    cosine, sine = rotary_tables(len_ref, table, rows)
 
     for i in range(blocks):
         w_copy(i).wait()
         part = jnp.dot(n_scr[...], wbuf[i % QKV_SLOTS], preferred_element_type=F32)
-        part = part + bias_ref[:, pl.ds(i * QKV_COLS, QKV_COLS)].astype(F32)
+        part = part + bias_ref[pl.ds(i * QKV_COLS, QKV_COLS)].astype(F32).reshape(1, -1)
         if i + QKV_SLOTS < blocks:
             w_copy(i + QKV_SLOTS).start()
         elif i + QKV_SLOTS - blocks < 2:
@@ -221,29 +234,34 @@
 
     contract_last = (((1,), (1,)), ((), ()))
 
-    def gate_up(j, carry):
-        slot = lax.rem(j, FF_SLOTS)
-        in_copy(j).wait()
-        gate = lax.dot_general(m_all[...], ring[slot, 0], contract_last, preferred_element_type=F32)
-        up = lax.dot_general(m_all[...], ring[slot, 1], contract_last, preferred_element_type=F32)
-        act[:, pl.ds(pl.multiple_of(j * FF_BLOCK, FF_BLOCK), FF_BLOCK)] = swiglu(gate, up)
-
-        @pl.when(j + FF_SLOTS < full)
-        def _():
-            in_copy(j + FF_SLOTS).start()
-
-        @pl.when(j + FF_SLOTS == full)
-        def _():
-            rest_copy().start()
+    def gate_up(t, carry):
+        for k in range(FF_UNROLL):
+            in_copy(t * FF_UNROLL + k).wait()
+        for k in range(FF_UNROLL):
+            j = t * FF_UNROLL + k
+            slot = lax.rem(j, FF_SLOTS)
+            gate = lax.dot_general(m_all[...], ring[slot, 0], contract_last, preferred_element_type=F32)
+            up = lax.dot_general(m_all[...], ring[slot, 1], contract_last, preferred_element_type=F32)
+            act[:, pl.ds(pl.multiple_of(j * FF_BLOCK, FF_BLOCK), FF_BLOCK)] = swiglu(gate, up)
+        for k in range(FF_UNROLL):
+            j = t * FF_UNROLL + k
+
+            @pl.when(j + FF_SLOTS < full)
+            def _():
+                in_copy(j + FF_SLOTS).start()
+
+            @pl.when(j + FF_SLOTS == full)
+            def _():
+                rest_copy().start()
 
         for c in range(2, OUT_SLOTS):
-            @pl.when(j == 3 * (c - 1))
+            @pl.when(t == c - 1)
             def _():
                 out_copy(c).start()
 
         return carry
 
-    lax.fori_loop(0, full, gate_up, 0)
+    lax.fori_loop(0, full // FF_UNROLL, gate_up, 0)
     rest_copy().wait()
     slot = full % FF_SLOTS
     gate = lax.dot_general(m_all[...], ring[slot, 0, pl.ds(0, rest), :], contract_last, preferred_element_type=F32)
@@ -310,23 +328,17 @@
         ffn = w_out.shape[0]
         cache_rows = cache_len * kv_heads
 
-        rot_dim = HEAD // 2
-        inv_freq = ROPE_BASE ** (-jnp.arange(0, rot_dim, 2, dtype=F32) / rot_dim)
-        angles = seq_len.astype(F32)[:, None] * jnp.repeat(inv_freq, 2)[None, :]
-        sign = jnp.where(jnp.arange(rot_dim) % 2 == 0, -1.0, 1.0).astype(F32)
-        cosine = jnp.concatenate([jnp.cos(angles), jnp.ones((rows, HEAD - rot_dim), F32)], axis=1)
-        sine = jnp.concatenate([jnp.sin(angles) * sign, jnp.zeros((rows, HEAD - rot_dim), F32)], axis=1)
-
         flat = jax.ShapeDtypeStruct((rows, cache_rows, HEAD), BF16)
         context, k_out, v_out = pl.pallas_call(
             functools.partial(qkv_attention_kernel, q_heads, kv_heads),
             out_shape=(jax.ShapeDtypeStruct((rows, HEAD_ROWS, HEAD), F32), flat, flat),
-            in_specs=[smem, vmem, vmem, vmem, vmem, vmem, hbm, hbm, hbm],
+            in_specs=[smem, vmem, vmem, vmem, hbm, hbm, hbm],
             out_specs=(vmem, hbm, hbm),
             scratch_shapes=[
                 pltpu.VMEM((QKV_SLOTS, width, QKV_COLS), BF16),
                 pltpu.VMEM((SEQ_SLOTS, SEQ_STEP, cache_rows, HEAD), BF16),
                 pltpu.VMEM((SEQ_SLOTS, SEQ_STEP, cache_rows, HEAD), BF16),
+                pltpu.VMEM((rows, HEAD), F32),
                 pltpu.VMEM((rows, width), BF16),
                 pltpu.VMEM((rows, HEAD_ROWS, HEAD), F32),
                 pltpu.VMEM((rows, 8, HEAD), F32),
@@ -335,7 +347,7 @@
             ],
             compiler_params=pltpu.CompilerParams(vmem_limit_bytes=60 * 1024 * 1024),
             name="qkv_attention",
-        )(seq_len, x_in, gamma_attn.reshape(1, width), b_qkv.reshape(1, -1), cosine, sine, w_qkv,
+        )(seq_len, x_in, gamma_attn, b_qkv, w_qkv,
           k_cache.reshape(rows, cache_rows, HEAD), v_cache.reshape(rows, cache_rows, HEAD))
 
         chunks = width // OUT_COLS
@@ -363,7 +375,7 @@
             compiler_params=pltpu.CompilerParams(collective_id=0, has_side_effects=True,
                                                  vmem_limit_bytes=67043328),
             name="proj_mlp",
-        )(context, x_in, gamma_mlp.reshape(1, width), w_proj.reshape(-1, FF_BLOCK, width), w_in, w_out)
+        )(context, x_in, gamma_mlp, w_proj.reshape(-1, FF_BLOCK, width), w_in, w_out)
         return layer_out, k_out.reshape(k_cache.shape), v_out.reshape(v_cache.shape)
 
     return jax.shard_map(local_layer, mesh=mesh,

time: 108 us -> 102 us (0.944)
  local copies, waits for them, and re-layouts: 7.16 us -> 1.82 us
    reshape x3 -> x0, local copies, waits for them, and re-layouts: 3.94 us -> none  [the longest x1 1.32 us: local_layer(): b_qkv.reshape(1, -1)]
    concatenate x2 -> x0, local copies, waits for them, and re-layouts: 1.24 us -> none  [the longest x1 0.62 us: local_layer(): jnp.concatenate([jnp.cos(angles), jnp.ones((rows, HEAD - rot_dim), F32)],...]
where the time goes in v2:
time: 102 us; the launch traced here: 101 us
  Pallas kernels  99 us (97%)
  local copies, waits for them, and re-layouts  1.82 us (2%)
    pallas_call x1, Pallas kernels, local_layer(): pl.pallas_call(functools.partial(mlp_kernel, q_heads), out_shape=jax.Shap...  63.3 us
    pallas_call x1, Pallas kernels, local_layer(): pl.pallas_call(functools.partial(qkv_attention_kernel, q_heads, kv_heads)...  35.7 us

profile of v2, /device:TPU:0, one launch (start us, length us, event | category | flops | bytes accessed | tf_op | source)
XLA Modules:
  0.0 101.5 jit_solution(214990813944941088)
XLA Ops:
  0.6 35.7 %qkv_attention.1 = (f32[64,32,128]{2,1,0:T(8,128)}, bf16[64,1024,128]{2,1,0:T(8,128)(2,1)}, bf16[64,1024,128]{2,1,0:T(8,128)(2,1)}) custom-call(s32[64]{0:T(128)} %len_ref.1, bf16[64,3584]{1,0:T(8,128)(2,1)} %x_ref.3, bf16[3584]{0:T(1024)(128)(2,1)} %gain_ref.2, bf16[4608]{0:T(1024)(128)(2,1)} %bias_ref.1, bf16[3584,4608]{1,0:T(8,128)(2,1)} %w_hbm.1, ...), custom_call_target="tpu_custom_call" | custom-call | tf_op jit(solution)/shard_map/qkv_attention/pallas_call | solution.py:332
  36.3 63.3 %proj_mlp.1 = bf16[64,3584]{1,0:T(8,128)(2,1)} custom-call(f32[64,32,128]{2,1,0:T(8,128)} %get-tuple-element.6.ctx_ref, bf16[64,3584]{1,0:T(8,128)(2,1)} %x_ref.3, bf16[3584]{0:T(1024)(128)(2,1)} %gain_ref.3, bf16[14,256,3584]{2,1,0:T(8,128)(2,1)} %bitcast.5, bf16[2,4736,3584]{2,1,0:T(8,128)(2,1)} %wi_hbm.1, bf16[4736,3584]{1,0:T(8,128)(2,1)} %wo_hbm.1), custom_call_target="tpu_custom_call" | custom-call | tf_op jit(solution)/shard_map/proj_mlp/pallas_call | solution.py:354
  99.6 1.8 %copy.15 = bf16[64,3584]{1,0:T(8,128)(2,1)} copy(bf16[64,3584]{1,0:T(8,128)(2,1)} %proj_mlp.1) | data formatting | bytes 917504

commit v3 on v2

--- a/solution.py
+++ b/solution.py
@@ -22,8 +22,8 @@
 SEQ_SLOTS = 4
 HEAD_ROWS = 32
 FF_BLOCK = 256
-FF_SLOTS = 7
-FF_UNROLL = 3
+FF_SLOTS = 8
+FF_GROUPS = (2, 3, 3, 2)
 OUT_COLS = 512
 OUT_SLOTS = 5
 AG_CHUNKS = 4
@@ -46,14 +46,20 @@
     return jnp.cos(angles), jnp.where(lax.rem(dim, 2) == 0, -sine, sine)
 
 
-def qkv_attention_kernel(q_heads, kv_heads, len_ref, x_ref, gain_ref, bias_ref, w_hbm, k_hbm, v_hbm,
-                         ctx_ref, ko_hbm, vo_hbm, wbuf, kbuf, vbuf, table, n_scr, q_scr, kn_scr, vn_scr,
-                         w_sem, ki_sem, vi_sem, ko_sem, vo_sem):
-    rows = x_ref.shape[0]
+def attention_kernel(q_heads, kv_heads, len_hbm, x_hbm, gain_hbm, bias_hbm, gain2_hbm, w_hbm, wp_hbm, k_hbm, v_hbm,
+                     m_ref, hid_ref, ko_hbm, vo_hbm,
+                     len_ref, x_ref, gain_ref, bias_ref, gain2_ref, wbuf, kbuf, vbuf, table, n_scr, q_scr, kn_scr, vn_scr,
+                     ctx_ref, small_sem, w_sem, ki_sem, vi_sem, ko_sem, vo_sem):
+    rows, width = x_ref.shape
     blocks = w_hbm.shape[1] // QKV_COLS
+    proj_blocks = wp_hbm.shape[1] // QKV_COLS
     steps = rows // SEQ_STEP
     group = q_heads // kv_heads
     heads_per_block = QKV_COLS // HEAD
+
+    def proj_copy(i):
+        return pltpu.make_async_copy(wp_hbm.at[:, pl.ds(i * QKV_COLS, QKV_COLS)], wbuf.at[i % QKV_SLOTS],
+                                     w_sem.at[i % QKV_SLOTS])
 
     def w_copy(i):
         return pltpu.make_async_copy(w_hbm.at[:, pl.ds(i * QKV_COLS, QKV_COLS)], wbuf.at[i % QKV_SLOTS],
@@ -71,10 +77,16 @@
         return (pltpu.make_async_copy(kbuf.at[slot], ko_hbm.at[part], ko_sem.at[slot]),
                 pltpu.make_async_copy(vbuf.at[slot], vo_hbm.at[part], vo_sem.at[slot]))
 
+    small = [pltpu.make_async_copy(src, dst, small_sem.at[i]) for i, (src, dst) in enumerate((
+        (x_hbm, x_ref), (gain_hbm, gain_ref), (len_hbm, len_ref), (bias_hbm, bias_ref), (gain2_hbm, gain2_ref)))]
+    for copy in small:
+        copy.start()
     for i in range(QKV_SLOTS):
-        w_copy(i).start()
+        w_copy(i).start(priority=1)
+    q_scr[:, pl.ds(q_heads, HEAD_ROWS - q_heads), :] = jnp.zeros((rows, HEAD_ROWS - q_heads, HEAD), F32)
+    for copy in small:
+        copy.wait()
     n_scr[...] = rms_norm(x_ref[...].astype(F32), gain_ref[...])
-    q_scr[:, pl.ds(q_heads, HEAD_ROWS - q_heads), :] = jnp.zeros((rows, HEAD_ROWS - q_heads, HEAD), F32)
     even = lax.rem(lax.broadcasted_iota(jnp.int32, (rows, HEAD), 1), 2) == 0
     cosine, sine = rotary_tables(len_ref, table, rows)
 
@@ -83,7 +95,7 @@
         part = jnp.dot(n_scr[...], wbuf[i % QKV_SLOTS], preferred_element_type=F32)
         part = part + bias_ref[pl.ds(i * QKV_COLS, QKV_COLS)].astype(F32).reshape(1, -1)
         if i + QKV_SLOTS < blocks:
-            w_copy(i + QKV_SLOTS).start()
+            w_copy(i + QKV_SLOTS).start(priority=1)
         elif i + QKV_SLOTS - blocks < 2:
             for copy in in_copies(i + QKV_SLOTS - blocks):
                 copy.start()
@@ -145,23 +157,37 @@
             ctx_ref[i * SEQ_STEP + s] = jnp.dot(probs, vbuf[slot, s], preferred_element_type=F32)
         for copy in out_copies(i):
             copy.start()
+        for n in range(QKV_SLOTS):
+            @pl.when(i == steps - QKV_SLOTS + n)
+            def _():
+                proj_copy(n).start(priority=1)
+
         return carry
 
     lax.fori_loop(0, steps, attend, 0)
+    for head in range(q_heads):
+        n_scr[:, pl.ds(head * HEAD, HEAD)] = ctx_ref[:, head, :].astype(BF16)
+    for i in range(proj_blocks):
+        cols = pl.ds(i * QKV_COLS, QKV_COLS)
+        proj_copy(i).wait()
+        part = jnp.dot(n_scr[...], wbuf[i % QKV_SLOTS], preferred_element_type=F32)
+        if i + QKV_SLOTS < proj_blocks:
+            proj_copy(i + QKV_SLOTS).start(priority=1)
+        hid_ref[:, cols] = x_ref[:, cols].astype(F32) + part
+    m_ref[...] = rms_norm(hid_ref[...], gain2_ref[...])
     for i in (steps - 2, steps - 1):
         for copy in out_copies(i):
             copy.wait()
 
 
-def mlp_kernel(q_heads, ctx_ref, x_ref, gain_ref, wp_hbm, wi_hbm, wo_hbm, y_ref,
-               ring, oring, m_all, ctx2, hid, act, send_d, recv_d, keep, send_i, recv_i,
-               ring_sem, oring_sem, agx_s, agx_r, agp_s, agp_r, fwd_s, fwd_r, rsd_s, rsd_r, rsi_s, rsi_r):
-    rows, width = x_ref.shape
+def mlp_kernel(m_hbm, hid_hbm, wi_hbm, wo_hbm, y_ref,
+               ring, oring, m_all, hid, act, send_d, recv_d, keep, send_i, recv_i,
+               m_sem, hid_sem, ring_sem, rest_sem, oring_sem, agx_s, agx_r, agp_s, agp_r, fwd_s, fwd_r, rsd_s, rsd_r, rsi_s, rsi_r):
+    rows, width = m_hbm.shape
     ffn = wo_hbm.shape[0]
     me = lax.axis_index("grp")
     partner = {"grp": me + 1 - 2 * lax.rem(me, 2)}
     cross = {"grp": lax.rem(me + 2, 4)}
-    proj_blocks = wp_hbm.shape[0] // 2
     full = ffn // FF_BLOCK
     rest = ffn - full * FF_BLOCK
     chunks = width // OUT_COLS
@@ -169,43 +195,31 @@
     barrier = pltpu.get_barrier_semaphore()
     for peer in (partner, cross):
         pl.semaphore_signal(barrier, inc=1, device_id=peer, device_id_type=MESH)
-
-    def proj_copy(i):
-        return pltpu.make_async_copy(wp_hbm.at[pl.ds(2 * i, 2)], ring.at[i], ring_sem.at[i])
 
     def in_copy(j):
         slot = lax.rem(j, FF_SLOTS)
         return pltpu.make_async_copy(wi_hbm.at[:, pl.ds(pl.multiple_of(j * FF_BLOCK, FF_BLOCK), FF_BLOCK), :],
                                      ring.at[slot], ring_sem.at[slot])
 
-    def rest_copy():
+    def rest_copies():
         slot = full % FF_SLOTS
-        return pltpu.make_async_copy(wi_hbm.at[:, pl.ds(full * FF_BLOCK, rest), :],
-                                     ring.at[slot, :, pl.ds(0, rest), :], ring_sem.at[slot])
+        return [pltpu.make_async_copy(wi_hbm.at[g, pl.ds(full * FF_BLOCK, rest), :],
+                                      ring.at[slot, 0, pl.ds(g * rest, rest), :], rest_sem.at[g]) for g in range(2)]
 
     def out_copy(c):
         slot = lax.rem(c, OUT_SLOTS)
         return pltpu.make_async_copy(wo_hbm.at[:, pl.ds(pl.multiple_of(c * OUT_COLS, OUT_COLS), OUT_COLS)],
                                      oring.at[slot], oring_sem.at[slot])
 
-    for i in range(proj_blocks):
-        proj_copy(i).start()
-    for head in range(q_heads):
-        ctx2[:, pl.ds(head * HEAD, HEAD)] = ctx_ref[:, head, :].astype(BF16)
-    hid[...] = x_ref[...].astype(F32)
-
-    def project(i, carry):
-        proj_copy(i).wait()
-        block = ring[i].reshape(2 * FF_BLOCK, width)
-        left = ctx2[:, pl.ds(pl.multiple_of(i * 2 * FF_BLOCK, 2 * FF_BLOCK), 2 * FF_BLOCK)]
-        hid[...] += jnp.dot(left, block, preferred_element_type=F32)
-        in_copy(i).start()
-        return carry
-
-    lax.fori_loop(0, proj_blocks, project, 0)
-    out_copy(0).start()
-    out_copy(1).start()
-    m_all[pl.ds(0, rows), :] = rms_norm(hid[...], gain_ref[...])
+    m_copy = pltpu.make_async_copy(m_hbm, m_all.at[pl.ds(rows, rows)], m_sem)
+    hid_copy = pltpu.make_async_copy(hid_hbm, hid, hid_sem)
+    m_copy.start()
+    for j in range(FF_SLOTS):
+        in_copy(j).start(priority=1)
+    out_copy(0).start(priority=1)
+    out_copy(1).start(priority=1)
+    hid_copy.start(priority=1)
+    m_copy.wait()
     pl.semaphore_wait(barrier, 2)
 
     piece = rows // AG_CHUNKS
@@ -214,59 +228,102 @@
         return pltpu.make_async_remote_copy(src_ref=src, dst_ref=dst, send_sem=send, recv_sem=recv,
                                             device_id=peer, device_id_type=MESH)
 
-    to_cross = [remote(m_all.at[pl.ds(k * piece, piece)], m_all.at[pl.ds(rows + k * piece, piece)],
+    to_cross = [remote(m_all.at[pl.ds(rows + k * piece, piece)], m_all.at[pl.ds(k * piece, piece)],
                        agx_s.at[k], agx_r.at[k], cross) for k in range(AG_CHUNKS)]
-    to_partner = remote(m_all.at[pl.ds(0, rows)], m_all.at[pl.ds(2 * rows, rows)], agp_s, agp_r, partner)
-    forward = [remote(m_all.at[pl.ds(rows + k * piece, piece)], m_all.at[pl.ds(3 * rows + k * piece, piece)],
+    to_partner = remote(m_all.at[pl.ds(rows, rows)], m_all.at[pl.ds(2 * rows, rows)], agp_s, agp_r, partner)
+    forward = [remote(m_all.at[pl.ds(k * piece, piece)], m_all.at[pl.ds(3 * rows + k * piece, piece)],
                       fwd_s.at[k], fwd_r.at[k], partner) for k in range(AG_CHUNKS)]
+
+    def swiglu(gate, up):
+        return (gate / (1.0 + jnp.exp(-gate)) * up).astype(BF16)
+
+    contract_last = (((1,), (1,)), ((), ()))
+
+    tiles = width // FF_BLOCK
+
+    def gate_up(j):
+        slot = lax.rem(j, FF_SLOTS)
+        gate = lax.dot_general(m_all[...], ring[slot, 0], contract_last, preferred_element_type=F32)
+        up = lax.dot_general(m_all[...], ring[slot, 1], contract_last, preferred_element_type=F32)
+        act[:, pl.ds(pl.multiple_of(j * FF_BLOCK, FF_BLOCK), FF_BLOCK)] = swiglu(gate, up)
+
+    def chip_rows(j):
+        cols = pl.ds(pl.multiple_of(j * FF_BLOCK, FF_BLOCK), FF_BLOCK)
+        left = m_all[pl.ds(rows, 2 * rows), :]
+        both = []
+        for g in range(2):
+            turned = []
+            for k in range(tiles):
+                tile = ring[j, g, :, pl.ds(k * FF_BLOCK, FF_BLOCK)].T
+                ring[j, g, :, pl.ds(k * FF_BLOCK, FF_BLOCK)] = tile
+                turned.append(tile)
+            both.append(jnp.dot(left, jnp.concatenate(turned, axis=0), preferred_element_type=F32))
+        act[pl.ds(rows, 2 * rows), cols] = swiglu(*both)
+
+    def other_rows(j):
+        cols = pl.ds(pl.multiple_of(j * FF_BLOCK, FF_BLOCK), FF_BLOCK)
+        left = jnp.concatenate([m_all[pl.ds(0, rows), :], m_all[pl.ds(3 * rows, rows), :]], axis=0)
+        both = []
+        for g in range(2):
+            turned = [ring[j, g, :, pl.ds(k * FF_BLOCK, FF_BLOCK)] for k in range(tiles)]
+            both.append(jnp.dot(left, jnp.concatenate(turned, axis=0), preferred_element_type=F32))
+        result = swiglu(*both)
+        act[pl.ds(0, rows), cols] = result[:rows]
+        act[pl.ds(3 * rows, rows), cols] = result[rows:]
+
     for copy in to_cross:
         copy.start()
     to_partner.start()
-    for k in range(AG_CHUNKS):
-        to_cross[k].wait_recv()
-        forward[k].start()
     to_partner.wait_recv()
+
+    def early(j, carry):
+        in_copy(j).wait()
+        chip_rows(j)
+        for k in range(AG_CHUNKS):
+            @pl.when(j == min(2 * k + 2, FF_SLOTS - 1))
+            def _():
+                to_cross[k].wait_recv()
+                forward[k].start()
+
+        return carry
+
+    lax.fori_loop(0, FF_SLOTS, early, 0)
     for k in range(AG_CHUNKS):
         forward[k].wait_recv()
 
-    def swiglu(gate, up):
-        return (gate / (1.0 + jnp.exp(-gate)) * up).astype(BF16)
-
-    contract_last = (((1,), (1,)), ((), ()))
-
-    def gate_up(t, carry):
-        for k in range(FF_UNROLL):
-            in_copy(t * FF_UNROLL + k).wait()
-        for k in range(FF_UNROLL):
-            j = t * FF_UNROLL + k
-            slot = lax.rem(j, FF_SLOTS)
-            gate = lax.dot_general(m_all[...], ring[slot, 0], contract_last, preferred_element_type=F32)
-            up = lax.dot_general(m_all[...], ring[slot, 1], contract_last, preferred_element_type=F32)
-            act[:, pl.ds(pl.multiple_of(j * FF_BLOCK, FF_BLOCK), FF_BLOCK)] = swiglu(gate, up)
-        for k in range(FF_UNROLL):
-            j = t * FF_UNROLL + k
-
-            @pl.when(j + FF_SLOTS < full)
-            def _():
-                in_copy(j + FF_SLOTS).start()
-
-            @pl.when(j + FF_SLOTS == full)
-            def _():
-                rest_copy().start()
-
-        for c in range(2, OUT_SLOTS):
-            @pl.when(t == c - 1)
-            def _():
-                out_copy(c).start()
-
+    def late(t, carry):
+        for k in range(2):
+            other_rows(2 * t + k)
+        for k in range(2):
+            in_copy(2 * t + k + FF_SLOTS).start(priority=1)
         return carry
 
-    lax.fori_loop(0, full // FF_UNROLL, gate_up, 0)
-    rest_copy().wait()
-    slot = full % FF_SLOTS
-    gate = lax.dot_general(m_all[...], ring[slot, 0, pl.ds(0, rest), :], contract_last, preferred_element_type=F32)
-    up = lax.dot_general(m_all[...], ring[slot, 1, pl.ds(0, rest), :], contract_last, preferred_element_type=F32)
-    act[:, pl.ds(full * FF_BLOCK, rest)] = swiglu(gate, up)
+    lax.fori_loop(0, FF_SLOTS // 2, late, 0)
+
+    first = FF_SLOTS
+    for count in FF_GROUPS:
+        for j in range(first, first + count):
+            in_copy(j).wait()
+        last = first + count == full
+        if last:
+            for copy in rest_copies():
+                copy.wait()
+        for j in range(first, first + count):
+            gate_up(j)
+        if last:
+            both = lax.dot_general(m_all[...], ring[full % FF_SLOTS, 0], contract_last, preferred_element_type=F32)
+            act[:, pl.ds(full * FF_BLOCK, rest)] = swiglu(both[:, :rest], both[:, rest:])
+        for j in range(first, first + count):
+            if j + FF_SLOTS < full:
+                in_copy(j + FF_SLOTS).start(priority=1)
+            elif j + FF_SLOTS == full:
+                for copy in rest_copies():
+                    copy.start(priority=1)
+        if first + FF_SLOTS <= full < first + count + FF_SLOTS:
+            for c in range(2, OUT_SLOTS):
+                out_copy(c).start(priority=1)
+        first += count
+    hid_copy.wait()
 
     def die_copy(c):
         return remote(send_d.at[c], recv_d.at[c], rsd_s.at[c], rsd_r.at[c], partner)
@@ -277,9 +334,8 @@
     def finish(c):
         cols = pl.ds(pl.multiple_of(c * OUT_COLS, OUT_COLS), OUT_COLS)
         die_copy(c).wait_recv()
-        chip_sum = keep[lax.rem(c, 2)] + recv_d[c].astype(F32)
-        send_i[c] = chip_sum[rows:].astype(BF16)
-        hid[:, cols] += chip_sum[:rows]
+        send_i[c] = (keep[lax.rem(c, 2), pl.ds(0, rows)] + recv_d[c, pl.ds(rows, rows)].astype(F32)).astype(BF16)
+        hid[:, cols] += keep[lax.rem(c, 2), pl.ds(rows, rows)] + recv_d[c, pl.ds(0, rows)].astype(F32)
         chip_copy(c).start()
 
     def down(c, carry):
@@ -288,7 +344,7 @@
 
         @pl.when(c + OUT_SLOTS < chunks)
         def _():
-            out_copy(c + OUT_SLOTS).start()
+            out_copy(c + OUT_SLOTS).start(priority=1)
 
         send_d[c] = part[2 * rows:].astype(BF16)
         keep[lax.rem(c, 2)] = part[:2 * rows]
@@ -317,7 +373,6 @@
     row_spec = P(('rep', 'grp'))
     repl_spec = P()
     vmem = pl.BlockSpec(memory_space=pltpu.VMEM)
-    smem = pl.BlockSpec(memory_space=pltpu.SMEM)
     hbm = pl.BlockSpec(memory_space=pl.ANY)
     dma = pltpu.SemaphoreType.DMA
 
@@ -329,12 +384,17 @@
         cache_rows = cache_len * kv_heads
 
         flat = jax.ShapeDtypeStruct((rows, cache_rows, HEAD), BF16)
-        context, k_out, v_out = pl.pallas_call(
-            functools.partial(qkv_attention_kernel, q_heads, kv_heads),
-            out_shape=(jax.ShapeDtypeStruct((rows, HEAD_ROWS, HEAD), F32), flat, flat),
-            in_specs=[smem, vmem, vmem, vmem, hbm, hbm, hbm],
-            out_specs=(vmem, hbm, hbm),
+        mlp_in, hidden, k_out, v_out = pl.pallas_call(
+            functools.partial(attention_kernel, q_heads, kv_heads),
+            out_shape=(jax.ShapeDtypeStruct((rows, width), BF16), jax.ShapeDtypeStruct((rows, width), F32), flat, flat),
+            in_specs=[hbm] * 9,
+            out_specs=(vmem, vmem, hbm, hbm),
             scratch_shapes=[
+                pltpu.SMEM((rows,), jnp.int32),
+                pltpu.VMEM((rows, width), BF16),
+                pltpu.VMEM((width,), BF16),
+                pltpu.VMEM((b_qkv.shape[0],), BF16),
+                pltpu.VMEM((width,), BF16),
                 pltpu.VMEM((QKV_SLOTS, width, QKV_COLS), BF16),
                 pltpu.VMEM((SEQ_SLOTS, SEQ_STEP, cache_rows, HEAD), BF16),
                 pltpu.VMEM((SEQ_SLOTS, SEQ_STEP, cache_rows, HEAD), BF16),
@@ -343,24 +403,24 @@
                 pltpu.VMEM((rows, HEAD_ROWS, HEAD), F32),
                 pltpu.VMEM((rows, 8, HEAD), F32),
                 pltpu.VMEM((rows, 8, HEAD), F32),
-                dma((QKV_SLOTS,)), dma((SEQ_SLOTS,)), dma((SEQ_SLOTS,)), dma((SEQ_SLOTS,)), dma((SEQ_SLOTS,)),
+                pltpu.VMEM((rows, HEAD_ROWS, HEAD), F32),
+                dma((5,)), dma((QKV_SLOTS,)), dma((SEQ_SLOTS,)), dma((SEQ_SLOTS,)), dma((SEQ_SLOTS,)), dma((SEQ_SLOTS,)),
             ],
             compiler_params=pltpu.CompilerParams(vmem_limit_bytes=60 * 1024 * 1024),
-            name="qkv_attention",
-        )(seq_len, x_in, gamma_attn, b_qkv, w_qkv,
+            name="attention",
+        )(seq_len, x_in, gamma_attn, b_qkv, gamma_mlp, w_qkv, w_proj,
           k_cache.reshape(rows, cache_rows, HEAD), v_cache.reshape(rows, cache_rows, HEAD))
 
         chunks = width // OUT_COLS
         layer_out = pl.pallas_call(
-            functools.partial(mlp_kernel, q_heads),
+            mlp_kernel,
             out_shape=jax.ShapeDtypeStruct((rows, width), BF16),
-            in_specs=[vmem, vmem, vmem, hbm, hbm, hbm],
+            in_specs=[hbm] * 4,
             out_specs=vmem,
             scratch_shapes=[
                 pltpu.VMEM((FF_SLOTS, 2, FF_BLOCK, width), BF16),
                 pltpu.VMEM((OUT_SLOTS, ffn, OUT_COLS), BF16),
                 pltpu.VMEM((4 * rows, width), BF16),
-                pltpu.VMEM((rows, width), BF16),
                 pltpu.VMEM((rows, width), F32),
                 pltpu.VMEM((4 * rows, ffn), BF16),
                 pltpu.VMEM((chunks, 2 * rows, OUT_COLS), BF16),
@@ -368,14 +428,14 @@
                 pltpu.VMEM((2, 2 * rows, OUT_COLS), F32),
                 pltpu.VMEM((chunks, rows, OUT_COLS), BF16),
                 pltpu.VMEM((chunks, rows, OUT_COLS), BF16),
-                dma((FF_SLOTS,)), dma((OUT_SLOTS,)),
+                dma, dma, dma((FF_SLOTS,)), dma((2,)), dma((OUT_SLOTS,)),
                 dma((AG_CHUNKS,)), dma((AG_CHUNKS,)), dma, dma, dma((AG_CHUNKS,)), dma((AG_CHUNKS,)),
                 dma((chunks,)), dma((chunks,)), dma((chunks,)), dma((chunks,)),
             ],
             compiler_params=pltpu.CompilerParams(collective_id=0, has_side_effects=True,
                                                  vmem_limit_bytes=67043328),
-            name="proj_mlp",
-        )(context, x_in, gamma_mlp, w_proj.reshape(-1, FF_BLOCK, width), w_in, w_out)
+            name="mlp",
+        )(mlp_in, hidden, w_in, w_out)
         return layer_out, k_out.reshape(k_cache.shape), v_out.reshape(v_cache.shape)
 
     return jax.shard_map(local_layer, mesh=mesh,

time: 102 us -> 100 us (0.980)
  Pallas kernels: 99 us -> 97.3 us
    pallas_call x2, Pallas kernels: 99 us -> 97.3 us  [the longest x1 52.7 us: local_layer(): pl.pallas_call(mlp_kernel, out_shape=jax.ShapeDtypeStruct((rows, width),...]
where the time goes in v3:
time: 100 us; the launch traced here: 99.8 us
  Pallas kernels  97.3 us (97%)
  local copies, waits for them, and re-layouts  1.82 us (2%)
    pallas_call x1, Pallas kernels, local_layer(): pl.pallas_call(mlp_kernel, out_shape=jax.ShapeDtypeStruct((rows, width),...  52.7 us
    pallas_call x1, Pallas kernels, local_layer(): pl.pallas_call(functools.partial(attention_kernel, q_heads, kv_heads), ou...  44.6 us

profile of v3, /device:TPU:0, one launch (start us, length us, event | category | flops | bytes accessed | tf_op | source)
XLA Modules:
  0.0 99.8 jit_solution(1268934763896841455)
XLA Ops:
  0.6 44.6 %attention.1 = (bf16[64,3584]{1,0:T(8,128)(2,1)}, f32[64,3584]{1,0:T(8,128)}, bf16[64,1024,128]{2,1,0:T(8,128)(2,1)}, bf16[64,1024,128]{2,1,0:T(8,128)(2,1)}) custom-call(s32[64]{0:T(128)} %len_hbm.1, bf16[64,3584]{1,0:T(8,128)(2,1)} %x_hbm.1, bf16[3584]{0:T(1024)(128)(2,1)} %gain_hbm.1, bf16[4608]{0:T(1024)(128)(2,1)} %bias_hbm.1, ...), custom_call_target="tpu_custom_call" | custom-call | tf_op jit(solution)/shard_map/attention/pallas_call | solution.py:387
  45.2 52.7 %mlp.1 = bf16[64,3584]{1,0:T(8,128)(2,1)} custom-call(bf16[64,3584]{1,0:T(8,128)(2,1)} %get-tuple-element.7.m_hbm, f32[64,3584]{1,0:T(8,128)} %get-tuple-element.8.hid_hbm, bf16[2,4736,3584]{2,1,0:T(8,128)(2,1)} %wi_hbm.1, bf16[4736,3584]{1,0:T(8,128)(2,1)} %wo_hbm.1), custom_call_target="tpu_custom_call" | custom-call | tf_op jit(solution)/shard_map/mlp/pallas_call | solution.py:415
  98.0 1.8 %copy.15 = bf16[64,3584]{1,0:T(8,128)(2,1)} copy(bf16[64,3584]{1,0:T(8,128)(2,1)} %mlp.1) | data formatting | bytes 917504

commit v4 on v3

--- a/solution.py
+++ b/solution.py
@@ -17,13 +17,13 @@
 LOG2E = 1.4426950408889634
 
 QKV_COLS = 512
-QKV_SLOTS = 4
+QKV_SLOTS = 6
+PROJ_AHEAD = 4
 SEQ_STEP = 4
 SEQ_SLOTS = 4
 HEAD_ROWS = 32
 FF_BLOCK = 256
 FF_SLOTS = 8
-FF_GROUPS = (2, 3, 3, 2)
 OUT_COLS = 512
 OUT_SLOTS = 5
 AG_CHUNKS = 4
@@ -58,8 +58,8 @@
     heads_per_block = QKV_COLS // HEAD
 
     def proj_copy(i):
-        return pltpu.make_async_copy(wp_hbm.at[:, pl.ds(i * QKV_COLS, QKV_COLS)], wbuf.at[i % QKV_SLOTS],
-                                     w_sem.at[i % QKV_SLOTS])
+        slot = (blocks + i) % QKV_SLOTS
+        return pltpu.make_async_copy(wp_hbm.at[:, pl.ds(i * QKV_COLS, QKV_COLS)], wbuf.at[slot], w_sem.at[slot])
 
     def w_copy(i):
         return pltpu.make_async_copy(w_hbm.at[:, pl.ds(i * QKV_COLS, QKV_COLS)], wbuf.at[i % QKV_SLOTS],
@@ -96,8 +96,10 @@
         part = part + bias_ref[pl.ds(i * QKV_COLS, QKV_COLS)].astype(F32).reshape(1, -1)
         if i + QKV_SLOTS < blocks:
             w_copy(i + QKV_SLOTS).start(priority=1)
-        elif i + QKV_SLOTS - blocks < 2:
-            for copy in in_copies(i + QKV_SLOTS - blocks):
+        elif i + QKV_SLOTS < blocks + PROJ_AHEAD:
+            proj_copy(i + QKV_SLOTS - blocks).start(priority=1)
+        if i >= blocks - 4 and i < blocks - 2:
+            for copy in in_copies(i + 4 - blocks):
                 copy.start()
         for j in range(heads_per_block):
             head = i * heads_per_block + j
@@ -157,20 +159,25 @@
             ctx_ref[i * SEQ_STEP + s] = jnp.dot(probs, vbuf[slot, s], preferred_element_type=F32)
         for copy in out_copies(i):
             copy.start()
-        for n in range(QKV_SLOTS):
-            @pl.when(i == steps - QKV_SLOTS + n)
+
+        @pl.when(lax.rem(i + 1, 16 // SEQ_STEP) == 0)
+        def _():
+            part = pl.ds(pl.multiple_of((i + 1) * SEQ_STEP - 16, 16), 16)
+            for head in range(q_heads):
+                n_scr[part, pl.ds(head * HEAD, HEAD)] = ctx_ref[part, head, :].astype(BF16)
+
+        for n in range(PROJ_AHEAD, QKV_SLOTS):
+            @pl.when(i == steps - 1 - QKV_SLOTS + n)
             def _():
                 proj_copy(n).start(priority=1)
 
         return carry
 
     lax.fori_loop(0, steps, attend, 0)
-    for head in range(q_heads):
-        n_scr[:, pl.ds(head * HEAD, HEAD)] = ctx_ref[:, head, :].astype(BF16)
     for i in range(proj_blocks):
         cols = pl.ds(i * QKV_COLS, QKV_COLS)
         proj_copy(i).wait()
-        part = jnp.dot(n_scr[...], wbuf[i % QKV_SLOTS], preferred_element_type=F32)
+        part = jnp.dot(n_scr[...], wbuf[(blocks + i) % QKV_SLOTS], preferred_element_type=F32)
         if i + QKV_SLOTS < proj_blocks:
             proj_copy(i + QKV_SLOTS).start(priority=1)
         hid_ref[:, cols] = x_ref[:, cols].astype(F32) + part
@@ -181,7 +188,7 @@
 
 
 def mlp_kernel(m_hbm, hid_hbm, wi_hbm, wo_hbm, y_ref,
-               ring, oring, m_all, hid, act, send_d, recv_d, keep, send_i, recv_i,
+               ring, rest_buf, oring, m_all, hid, act, send_d, recv_d, keep, send_i, recv_i,
                m_sem, hid_sem, ring_sem, rest_sem, oring_sem, agx_s, agx_r, agp_s, agp_r, fwd_s, fwd_r, rsd_s, rsd_r, rsi_s, rsi_r):
     rows, width = m_hbm.shape
     ffn = wo_hbm.shape[0]
@@ -201,10 +208,8 @@
         return pltpu.make_async_copy(wi_hbm.at[:, pl.ds(pl.multiple_of(j * FF_BLOCK, FF_BLOCK), FF_BLOCK), :],
                                      ring.at[slot], ring_sem.at[slot])
 
-    def rest_copies():
-        slot = full % FF_SLOTS
-        return [pltpu.make_async_copy(wi_hbm.at[g, pl.ds(full * FF_BLOCK, rest), :],
-                                      ring.at[slot, 0, pl.ds(g * rest, rest), :], rest_sem.at[g]) for g in range(2)]
+    rest_copies = [pltpu.make_async_copy(wi_hbm.at[g, pl.ds(full * FF_BLOCK, rest), :],
+                                         rest_buf.at[pl.ds(g * rest, rest), :], rest_sem.at[g]) for g in range(2)]
 
     def out_copy(c):
         slot = lax.rem(c, OUT_SLOTS)
@@ -216,8 +221,6 @@
     m_copy.start()
     for j in range(FF_SLOTS):
         in_copy(j).start(priority=1)
-    out_copy(0).start(priority=1)
-    out_copy(1).start(priority=1)
     hid_copy.start(priority=1)
     m_copy.wait()
     pl.semaphore_wait(barrier, 2)
@@ -247,29 +250,37 @@
         up = lax.dot_general(m_all[...], ring[slot, 1], contract_last, preferred_element_type=F32)
         act[:, pl.ds(pl.multiple_of(j * FF_BLOCK, FF_BLOCK), FF_BLOCK)] = swiglu(gate, up)
 
-    def chip_rows(j):
-        cols = pl.ds(pl.multiple_of(j * FF_BLOCK, FF_BLOCK), FF_BLOCK)
-        left = m_all[pl.ds(rows, 2 * rows), :]
-        both = []
-        for g in range(2):
-            turned = []
-            for k in range(tiles):
-                tile = ring[j, g, :, pl.ds(k * FF_BLOCK, FF_BLOCK)].T
-                ring[j, g, :, pl.ds(k * FF_BLOCK, FF_BLOCK)] = tile
-                turned.append(tile)
-            both.append(jnp.dot(left, jnp.concatenate(turned, axis=0), preferred_element_type=F32))
-        act[pl.ds(rows, 2 * rows), cols] = swiglu(*both)
-
-    def other_rows(j):
-        cols = pl.ds(pl.multiple_of(j * FF_BLOCK, FF_BLOCK), FF_BLOCK)
-        left = jnp.concatenate([m_all[pl.ds(0, rows), :], m_all[pl.ds(3 * rows, rows), :]], axis=0)
-        both = []
-        for g in range(2):
-            turned = [ring[j, g, :, pl.ds(k * FF_BLOCK, FF_BLOCK)] for k in range(tiles)]
-            both.append(jnp.dot(left, jnp.concatenate(turned, axis=0), preferred_element_type=F32))
-        result = swiglu(*both)
+    def transpose_tiles(ref):
+        tiles = []
+        for k in range(width // FF_BLOCK):
+            tile = ref[:, pl.ds(k * FF_BLOCK, FF_BLOCK)].T
+            ref[:, pl.ds(k * FF_BLOCK, FF_BLOCK)] = tile
+            tiles.append(tile)
+        return jnp.concatenate(tiles, axis=0)
+
+    def transposed_tiles(ref):
+        return jnp.concatenate([ref[:, pl.ds(k * FF_BLOCK, FF_BLOCK)] for k in range(width // FF_BLOCK)], axis=0)
+
+    def chip_rows():
+        return m_all[pl.ds(rows, 2 * rows), :]
+
+    def other_rows():
+        return jnp.concatenate([m_all[pl.ds(0, rows), :], m_all[pl.ds(3 * rows, rows), :]], axis=0)
+
+    def store_chip(cols, result):
+        act[pl.ds(rows, 2 * rows), cols] = result
+
+    def store_other(cols, result):
         act[pl.ds(0, rows), cols] = result[:rows]
         act[pl.ds(3 * rows, rows), cols] = result[rows:]
+
+    def half_rows(j, tiles, left, store):
+        gate, up = (jnp.dot(left(), tiles(ring.at[j, g]), preferred_element_type=F32) for g in range(2))
+        store(pl.ds(pl.multiple_of(j * FF_BLOCK, FF_BLOCK), FF_BLOCK), swiglu(gate, up))
+
+    def half_rows_rest(tiles, left, store):
+        both = jnp.dot(left(), tiles(rest_buf), preferred_element_type=F32)
+        store(pl.ds(full * FF_BLOCK, rest), swiglu(both[:, :rest], both[:, rest:]))
 
     for copy in to_cross:
         copy.start()
@@ -278,9 +289,20 @@
 
     def early(j, carry):
         in_copy(j).wait()
-        chip_rows(j)
-        for k in range(AG_CHUNKS):
-            @pl.when(j == min(2 * k + 2, FF_SLOTS - 1))
+        half_rows(j, transpose_tiles, chip_rows, store_chip)
+
+        @pl.when(j == 1)
+        def _():
+            for copy in rest_copies:
+                copy.start(priority=1)
+
+        for c in range(2):
+            @pl.when(j == 2 * c + 2)
+            def _():
+                out_copy(c).start(priority=1)
+
+        for k in range(AG_CHUNKS - 1):
+            @pl.when(j == 2 * k + 2)
             def _():
                 to_cross[k].wait_recv()
                 forward[k].start()
@@ -288,41 +310,43 @@
         return carry
 
     lax.fori_loop(0, FF_SLOTS, early, 0)
+    for copy in rest_copies:
+        copy.wait()
+    half_rows_rest(transpose_tiles, chip_rows, store_chip)
+    to_cross[AG_CHUNKS - 1].wait_recv()
+    forward[AG_CHUNKS - 1].start()
     for k in range(AG_CHUNKS):
         forward[k].wait_recv()
 
     def late(t, carry):
         for k in range(2):
-            other_rows(2 * t + k)
+            half_rows(2 * t + k, transposed_tiles, other_rows, store_other)
         for k in range(2):
             in_copy(2 * t + k + FF_SLOTS).start(priority=1)
         return carry
 
     lax.fori_loop(0, FF_SLOTS // 2, late, 0)
-
-    first = FF_SLOTS
-    for count in FF_GROUPS:
-        for j in range(first, first + count):
-            in_copy(j).wait()
-        last = first + count == full
-        if last:
-            for copy in rest_copies():
-                copy.wait()
-        for j in range(first, first + count):
-            gate_up(j)
-        if last:
-            both = lax.dot_general(m_all[...], ring[full % FF_SLOTS, 0], contract_last, preferred_element_type=F32)
-            act[:, pl.ds(full * FF_BLOCK, rest)] = swiglu(both[:, :rest], both[:, rest:])
-        for j in range(first, first + count):
-            if j + FF_SLOTS < full:
-                in_copy(j + FF_SLOTS).start(priority=1)
-            elif j + FF_SLOTS == full:
-                for copy in rest_copies():
-                    copy.start(priority=1)
-        if first + FF_SLOTS <= full < first + count + FF_SLOTS:
-            for c in range(2, OUT_SLOTS):
+    half_rows_rest(transposed_tiles, other_rows, store_other)
+
+    def main(t, carry):
+        for k in range(2):
+            in_copy(FF_SLOTS + 2 * t + k).wait()
+        for k in range(2):
+            gate_up(FF_SLOTS + 2 * t + k)
+
+        @pl.when(t == 0)
+        def _():
+            for j in range(2 * FF_SLOTS, full):
+                in_copy(j).start(priority=1)
+
+        for c in range(2, OUT_SLOTS):
+            @pl.when(t == c)
+            def _():
                 out_copy(c).start(priority=1)
-        first += count
+
+        return carry
+
+    lax.fori_loop(0, (full - FF_SLOTS) // 2, main, 0)
     hid_copy.wait()
 
     def die_copy(c):
@@ -419,6 +443,7 @@
             out_specs=vmem,
             scratch_shapes=[
                 pltpu.VMEM((FF_SLOTS, 2, FF_BLOCK, width), BF16),
+                pltpu.VMEM((FF_BLOCK, width), BF16),
                 pltpu.VMEM((OUT_SLOTS, ffn, OUT_COLS), BF16),
                 pltpu.VMEM((4 * rows, width), BF16),
                 pltpu.VMEM((rows, width), F32),

time: 100 us -> 94.4 us (0.944)
  Pallas kernels: 97.3 us -> 91.8 us
    pallas_call x1, Pallas kernels: 52.7 us -> 48.6 us  [local_layer(): pl.pallas_call(mlp_kernel, out_shape=jax.ShapeDtypeStruct((rows, width),...]
    pallas_call x1, Pallas kernels: 44.6 us -> 43.2 us  [local_layer(): pl.pallas_call(functools.partial(attention_kernel, q_heads, kv_heads), ou...]
where the time goes in v4:
time: 94.4 us; the launch traced here: 94.3 us
  Pallas kernels  91.8 us (97%)
  local copies, waits for them, and re-layouts  1.82 us (2%)
    pallas_call x1, Pallas kernels, local_layer(): pl.pallas_call(mlp_kernel, out_shape=jax.ShapeDtypeStruct((rows, width),...  48.6 us
    pallas_call x1, Pallas kernels, local_layer(): pl.pallas_call(functools.partial(attention_kernel, q_heads, kv_heads), ou...  43.2 us

profile of v4, /device:TPU:0, one launch (start us, length us, event | category | flops | bytes accessed | tf_op | source)
XLA Modules:
  0.0 94.3 jit_solution(1389293236555532662)
XLA Ops:
  0.6 43.2 %attention.1 = (bf16[64,3584]{1,0:T(8,128)(2,1)}, f32[64,3584]{1,0:T(8,128)}, bf16[64,1024,128]{2,1,0:T(8,128)(2,1)}, bf16[64,1024,128]{2,1,0:T(8,128)(2,1)}) custom-call(s32[64]{0:T(128)} %len_hbm.1, bf16[64,3584]{1,0:T(8,128)(2,1)} %x_hbm.1, bf16[3584]{0:T(1024)(128)(2,1)} %gain_hbm.1, bf16[4608]{0:T(1024)(128)(2,1)} %bias_hbm.1, ...), custom_call_target="tpu_custom_call" | custom-call | tf_op jit(solution)/shard_map/attention/pallas_call | solution.py:411
  43.8 48.6 %mlp.1 = bf16[64,3584]{1,0:T(8,128)(2,1)} custom-call(bf16[64,3584]{1,0:T(8,128)(2,1)} %get-tuple-element.7.m_hbm, f32[64,3584]{1,0:T(8,128)} %get-tuple-element.8.hid_hbm, bf16[2,4736,3584]{2,1,0:T(8,128)(2,1)} %wi_hbm.1, bf16[4736,3584]{1,0:T(8,128)(2,1)} %wo_hbm.1), custom_call_target="tpu_custom_call" | custom-call | tf_op jit(solution)/shard_map/mlp/pallas_call | solution.py:439
  92.4 1.8 %copy.15 = bf16[64,3584]{1,0:T(8,128)(2,1)} copy(bf16[64,3584]{1,0:T(8,128)(2,1)} %mlp.1) | data formatting | bytes 917504

commit v5 on v4

--- a/solution.py
+++ b/solution.py
@@ -17,9 +17,10 @@
 LOG2E = 1.4426950408889634
 
 QKV_COLS = 512
-QKV_SLOTS = 6
-PROJ_AHEAD = 4
-SEQ_STEP = 4
+QKV_SLOTS = 7
+PROJ_GROUP = 2
+PROJ_AHEAD = 3
+SEQ_STEP = 8
 SEQ_SLOTS = 4
 HEAD_ROWS = 32
 FF_BLOCK = 256
@@ -167,20 +168,23 @@
                 n_scr[part, pl.ds(head * HEAD, HEAD)] = ctx_ref[part, head, :].astype(BF16)
 
         for n in range(PROJ_AHEAD, QKV_SLOTS):
-            @pl.when(i == steps - 1 - QKV_SLOTS + n)
+            @pl.when(i == steps - 1 - (QKV_SLOTS - n) // 2)
             def _():
                 proj_copy(n).start(priority=1)
 
         return carry
 
     lax.fori_loop(0, steps, attend, 0)
-    for i in range(proj_blocks):
-        cols = pl.ds(i * QKV_COLS, QKV_COLS)
-        proj_copy(i).wait()
-        part = jnp.dot(n_scr[...], wbuf[(blocks + i) % QKV_SLOTS], preferred_element_type=F32)
-        if i + QKV_SLOTS < proj_blocks:
-            proj_copy(i + QKV_SLOTS).start(priority=1)
-        hid_ref[:, cols] = x_ref[:, cols].astype(F32) + part
+    for first in range(0, proj_blocks, PROJ_GROUP):
+        group_blocks = range(first, min(first + PROJ_GROUP, proj_blocks))
+        for i in group_blocks:
+            proj_copy(i).wait()
+        parts = [jnp.dot(n_scr[...], wbuf[(blocks + i) % QKV_SLOTS], preferred_element_type=F32) for i in group_blocks]
+        for i in group_blocks:
+            if i + QKV_SLOTS < proj_blocks:
+                proj_copy(i + QKV_SLOTS).start(priority=1)
+            cols = pl.ds(i * QKV_COLS, QKV_COLS)
+            hid_ref[:, cols] = x_ref[:, cols].astype(F32) + parts[i - first]
     m_ref[...] = rms_norm(hid_ref[...], gain2_ref[...])
     for i in (steps - 2, steps - 1):
         for copy in out_copies(i):

time: 94.4 us -> 93.4 us (0.989)
  Pallas kernels: 91.8 us -> 90.8 us
    pallas_call x1, Pallas kernels: 43.2 us -> 42.2 us  [local_layer(): pl.pallas_call(functools.partial(attention_kernel, q_heads, kv_heads), ou...]
where the time goes in v5:
time: 93.4 us; the launch traced here: 93.3 us
  Pallas kernels  90.8 us (97%)
  local copies, waits for them, and re-layouts  1.82 us (2%)
    pallas_call x1, Pallas kernels, local_layer(): pl.pallas_call(mlp_kernel, out_shape=jax.ShapeDtypeStruct((rows, width),...  48.6 us
    pallas_call x1, Pallas kernels, local_layer(): pl.pallas_call(functools.partial(attention_kernel, q_heads, kv_heads), ou...  42.2 us

profile of v5, /device:TPU:0, one launch (start us, length us, event | category | flops | bytes accessed | tf_op | source)
XLA Modules:
  0.0 93.3 jit_solution(1417876134422668291)
XLA Ops:
  0.6 42.2 %attention.1 = (bf16[64,3584]{1,0:T(8,128)(2,1)}, f32[64,3584]{1,0:T(8,128)}, bf16[64,1024,128]{2,1,0:T(8,128)(2,1)}, bf16[64,1024,128]{2,1,0:T(8,128)(2,1)}) custom-call(s32[64]{0:T(128)} %len_hbm.1, bf16[64,3584]{1,0:T(8,128)(2,1)} %x_hbm.1, bf16[3584]{0:T(1024)(128)(2,1)} %gain_hbm.1, bf16[4608]{0:T(1024)(128)(2,1)} %bias_hbm.1, ...), custom_call_target="tpu_custom_call" | custom-call | tf_op jit(solution)/shard_map/attention/pallas_call | solution.py:415
  42.8 48.6 %mlp.1 = bf16[64,3584]{1,0:T(8,128)(2,1)} custom-call(bf16[64,3584]{1,0:T(8,128)(2,1)} %get-tuple-element.7.m_hbm, f32[64,3584]{1,0:T(8,128)} %get-tuple-element.8.hid_hbm, bf16[2,4736,3584]{2,1,0:T(8,128)(2,1)} %wi_hbm.1, bf16[4736,3584]{1,0:T(8,128)(2,1)} %wo_hbm.1), custom_call_target="tpu_custom_call" | custom-call | tf_op jit(solution)/shard_map/mlp/pallas_call | solution.py:443
  91.5 1.8 %copy.15 = bf16[64,3584]{1,0:T(8,128)(2,1)} copy(bf16[64,3584]{1,0:T(8,128)(2,1)} %mlp.1) | data formatting | bytes 917504
